TPU v7x, 8 devices: a whole 2x2x1 slice. The times are simulated.
8 devices in a mesh: dp: 1 (over z), tp: 8 (over x, y, core).
Axes of the slice: x: 2, y: 2, z: 1, core: 2. Of those that a mesh axis runs over, the one named last changes fastest.
Arguments:
- x: bfloat16 [2816, 3072], P(('dp', 'tp'))
- w_gate: bfloat16 [3072, 24576], P(None, 'tp')
- w_up: bfloat16 [3072, 24576], P(None, 'tp')
- w_down: bfloat16 [24576, 3072], P('tp')
Outputs:
- output: bfloat16 [2816, 3072], P(('dp', 'tp'))
All inputs are finite; a program needn't handle non-finite values.
Results may differ from a plain program's by a relative error of at most 0.016.
Values are sent between devices in bfloat16 or wider.
A program may use at most 2 GiB of HBM per device.

v0:
```python
import jax
import jax.numpy as jnp
from jax import lax
from jax.sharding import PartitionSpec as P


def solution(mesh):
    def step(x, w_gate, w_up, w_down):
        rows = lax.all_gather(x, "tp", axis=0, tiled=True)
        gate = jnp.dot(rows, w_gate, preferred_element_type=jnp.float32)
        up = jnp.dot(rows, w_up, preferred_element_type=jnp.float32)
        hidden = (jax.nn.gelu(gate) * up).astype(jnp.bfloat16)
        term = jnp.dot(hidden, w_down, preferred_element_type=jnp.float32).astype(jnp.bfloat16)
        return lax.psum_scatter(term, "tp", scatter_dimension=0, tiled=True)

    return jax.shard_map(
        step,
        mesh=mesh,
        in_specs=(P(("dp", "tp"), None), P(None, "tp"), P(None, "tp"), P("tp", None)),
        out_specs=P(("dp", "tp"), None),
        check_vma=False,
    )
```

profile of v0, /device:TPU:0, one launch (start us, length us, event | category | flops | bytes accessed | tf_op | source)
XLA Modules:
  0.0 414.2 jit_solution(16179721548004235216)
XLA Ops:
  6.5 0.0 all-gather.2.cloned.1.call-start
  6.5 0.7 all-gather.2.cloned.1.call-update
  7.3 0.0 reduce-scatter.2.cloned.1.call-start
  7.3 91.0 %all-gather.2.cloned.1.call-done = bf16[2816,3072]{1,0:T(8,128)(2,1)} async-done(((bf16[352,3072]{1,0:T(8,128)(2,1)}), bf16[2816,3072]{1,0:T(8,128)(2,1)}) %all-gather.2.cloned.1.call-update) | async-done | bytes 17301520 | tf_op jit(solution)/shard_map/all_gather | solution.py:9
  98.3 62.6 %fusion.9 = f32[2816,3072]{1,0:T(8,128)} fusion(bf16[2816,3072]{1,0:T(8,128)(2,1)} %all-gather.2.cloned.1.call-done, bf16[3072,3072]{1,0:T(8,128)(2,1)} %param.5), kind=kOutput, calls=%fused_computation.11 | convolution fusion | flops 53150220288 | bytes 70778880 | tf_op jit(solution)/shard_map/dot_general | solution.py:10
  160.9 74.0 %fusion.8 = bf16[2816,3072]{1,0:T(8,128)(2,1)} fusion(f32[2816,3072]{1,0:T(8,128)} %fusion.9, bf16[2816,3072]{1,0:T(8,128)(2,1)} %all-gather.2.cloned.1.call-done, bf16[3072,3072]{1,0:T(8,128)(2,1)} %param.6), kind=kOutput, calls=%fused_computation.9 | convolution fusion | flops 53236727808 | bytes 88080384 | tf_op jit(solution)/shard_map/dot_general | solution.py:11
  234.9 62.7 %convolution_convert_fusion = bf16[2816,3072]{1,0:T(8,128)(2,1)} fusion(bf16[2816,3072]{1,0:T(8,128)(2,1)} %fusion.8, bf16[3072,3072]{1,0:T(8,128)(2,1)} %param.7), kind=kOutput, calls=%fused_computation.10 | convolution fusion | flops 53158871040 | bytes 53477376 | tf_op jit(solution)/shard_map/dot_general | solution.py:13
  297.6 0.0 reduce-scatter.2.cloned.1.call-update
  297.6 109.7 %reduce-scatter.2.cloned.1.call-done = bf16[352,3072]{1,0:T(8,128)(2,1)} async-done(((bf16[2816,3072]{1,0:T(8,128)(2,1)}), bf16[352,3072]{1,0:T(8,128)(2,1)}) %reduce-scatter.2.cloned.1.call-update) | async-done | bytes 2162704 | tf_op jit(solution)/shard_map/reduce_scatter | solution.py:14
Async XLA Ops:
  6.5 91.8 %all-gather.2.cloned.1.call-start = ((), (), s32[]{:S(2)}) async-start(), calls=%async_computation.1 | async-start | bytes 19464192 | tf_op jit(solution)/shard_map/all_gather | solution.py:9
  7.3 400.1 %reduce-scatter.2.cloned.1.call-start = ((), (), s32[]{:S(2)}) async-start(), calls=%async_computation.2 | async-start | bytes 19464192 | tf_op jit(solution)/shard_map/reduce_scatter | solution.py:14
Sparse Core Ops, SparseCore 0:
  9.1 89.1 all-gather.1
  297.8 109.5 reduce-scatter.1
where the time goes:
time: 414 us
  waiting for transfers between devices  201 us (49%)
  matrix products  199 us (48%)
  between operations  13.4 us (3%)
    reduce_scatter x1, waiting for transfers between devices, step(): return lax.psum_scatter(term, 'tp', scatter_dimension=0, tiled=True)  110 us
    all_gather x1, waiting for transfers between devices, step(): rows = lax.all_gather(x, 'tp', axis=0, tiled=True)  91 us
    dot_general x1, matrix products, step(): up = jnp.dot(rows, w_up, preferred_element_type=jnp.float32)  74 us
    dot_general x1, matrix products, step(): jnp.dot(hidden, w_down, preferred_element_type=jnp.float32)  62.7 us
    dot_general x1, matrix products, step(): gate = jnp.dot(rows, w_gate, preferred_element_type=jnp.float32)  62.6 us
  transfers between devices with their start and end apart: 2, of which 2 were waited for; matrix products, arithmetic and copies ran while one was open for 0% of the time, Pallas kernels for 0%

commit v1 on v0

v1 whole, which is shorter than its diff:
```python
import jax
import jax.numpy as jnp
from jax import lax
from jax.experimental import pallas as pl
from jax.experimental.pallas import tpu as pltpu
from jax.sharding import PartitionSpec as P

ROWS = 352
HALF = 176
D = 3072
FF = 3072
N1 = 256
N2 = 512
T1, T2 = FF // N1, D // N2
R1, R2 = 3, 3
SLOTS = 5
BF16, F32 = jnp.bfloat16, jnp.float32


def kernel(
    x_hbm, wg, wu, wd, y_hbm,
    xo, xp, xg, h, bg, bu, bd, acc, own, psend, precv, rbuf,
    s_x, s_g, s_u, s_d, s_y,
    ag_s, ag_r, fw_s, fw_r, ps_s, ps_r, rs_s, rs_r,
):
    dp = lax.axis_index("dp")
    me = lax.axis_index("tp")
    k, iy, ix = lax.rem(me, 2), lax.rem(me // 2, 2), me // 4
    partner = me + 1 - 2 * k
    ynbr = me + 2 - 4 * iy
    xnbr = me + 4 - 8 * ix
    dnbr = xnbr + 2 - 4 * iy

    def remote(src, dst, ss, rs, dev):
        return pltpu.make_async_remote_copy(
            src_ref=src, dst_ref=dst, send_sem=ss, recv_sem=rs,
            device_id=(dp, dev), device_id_type=pl.DeviceIdType.MESH,
        )

    def gu_copies(kk):
        t, r = lax.rem(kk, T1), lax.rem(kk, R1)
        cols = pl.ds(pl.multiple_of(t * N1, N1), N1)
        return (
            pltpu.make_async_copy(wg.at[:, cols], bg.at[r], s_g.at[r]),
            pltpu.make_async_copy(wu.at[:, cols], bu.at[r], s_u.at[r]),
        )

    def d_copy(kk):
        t, r = lax.rem(kk, T2), lax.rem(kk, R2)
        cols = pl.ds(pl.multiple_of(t * N2, N2), N2)
        return pltpu.make_async_copy(wd.at[:, cols], bd.at[r], s_d.at[r])

    top, bot = pl.ds(0, HALF), pl.ds(HALF, HALF)
    to_partner = lambda: remote(x_hbm, xp, ag_s.at[0], ag_r.at[0], partner)
    x_first = lambda: remote(x_hbm.at[top], xg.at[0, top], ag_s.at[1], ag_r.at[1], xnbr)
    y_first = lambda: remote(x_hbm.at[bot], xg.at[0, bot], ag_s.at[2], ag_r.at[2], ynbr)
    relay_y = lambda: remote(xg.at[0, top], xg.at[1, top], ag_s.at[3], ag_r.at[3], ynbr)
    relay_x = lambda: remote(xg.at[0, bot], xg.at[1, bot], ag_s.at[4], ag_r.at[4], xnbr)
    x_second = lambda: remote(x_hbm.at[bot], xg.at[2, top], ag_s.at[5], ag_r.at[5], xnbr)
    y_second = lambda: remote(x_hbm.at[top], xg.at[2, bot], ag_s.at[6], ag_r.at[6], ynbr)

    def forward(s):
        return remote(
            xg.at[s, pl.ds(0, ROWS)], xg.at[s, pl.ds(ROWS, ROWS)], fw_s.at[s], fw_r.at[s], partner
        )

    def to_core(par, n):
        return remote(psend.at[n], precv.at[par, n], ps_s.at[n], ps_r.at[par, n], partner)

    def to_owner(s, n, sub):
        dev = dnbr if s == 1 else (xnbr if sub == 0 else ynbr)
        row = HALF * (sub if s < 2 else 1 - sub)
        cols = pl.ds(pl.multiple_of(n * N2, N2), N2)
        return remote(
            xg.at[s, pl.ds(ROWS + HALF * sub, HALF), cols],
            rbuf.at[s, n, pl.ds(row, HALF)],
            rs_s.at[s, sub, n], rs_r.at[s, sub, n], dev,
        )

    def lag(s, n):
        par = lax.rem(s, 2)
        to_core(par, n).wait_recv()
        total = own[lax.rem(n, 3)] + precv[par, n].astype(F32)
        xg[s, pl.ds(ROWS, ROWS), pl.ds(pl.multiple_of(n * N2, N2), N2)] = total.astype(BF16)
        for ss in range(3):
            @pl.when(s == ss)
            def _():
                to_owner(ss, n, 0).start()
                to_owner(ss, n, 1).start()

    def phase1(si, x_ref, rows, hook):
        def step(t, _):
            kk = si * T1 + t
            r = lax.rem(kk, R1)
            for c in gu_copies(kk):
                c.wait()

            @pl.when(kk + R1 - 1 < SLOTS * T1)
            def _():
                for c in gu_copies(kk + R1 - 1):
                    c.start()

            hook(t)
            gate = jnp.dot(x_ref[...], bg[r], preferred_element_type=F32)
            up = jnp.dot(x_ref[...], bu[r], preferred_element_type=F32)
            cols = pl.ds(pl.multiple_of(t * N1, N1), N1)
            h[pl.ds(0, rows), cols] = (jax.nn.gelu(gate) * up).astype(BF16)
            return 0

        lax.fori_loop(0, T1, step, 0)

    def phase2(si, rows, before, after):
        def step(n, _):
            kk = si * T2 + n
            d_copy(kk).wait()

            @pl.when(kk + R2 - 1 < SLOTS * T2)
            def _():
                d_copy(kk + R2 - 1).start()

            before(n)
            p = jnp.dot(h[pl.ds(0, rows), :], bd[lax.rem(kk, R2)], preferred_element_type=F32)
            after(n, p)
            return 0

        lax.fori_loop(0, T2, step, 0)

    x_in = pltpu.make_async_copy(x_hbm, xo, s_x)
    x_in.start()
    for i in range(R1 - 1):
        for c in gu_copies(i):
            c.start()
    barrier = pltpu.get_barrier_semaphore()
    for dev in (partner, xnbr, ynbr, dnbr):
        pl.semaphore_signal(
            barrier, inc=1, device_id=(dp, dev), device_id_type=pl.DeviceIdType.MESH
        )
    pl.semaphore_wait(barrier, 4)
    x_first().start()
    y_first().start()
    to_partner().start()
    x_in.wait()

    def hook0(t):
        @pl.when(t == 0)
        def _():
            for i in range(R2 - 1):
                d_copy(i).start()

    phase1(0, xo, ROWS, hook0)

    def after0(n, p):
        acc[n] = p

    phase2(0, ROWS, lambda n: None, after0)

    x_first().wait_recv()
    y_first().wait_recv()
    forward(0).start()
    relay_y().start()
    relay_x().start()
    x_second().start()
    y_second().start()

    def big(s, _):
        forward(s).wait_recv()

        def hook(t):
            @pl.when((t == 1) & (s > 0))
            def _():
                lag(s - 1, T2 - 2)
                lag(s - 1, T2 - 1)

        phase1(s + 1, xg.at[s], 2 * ROWS, hook)

        @pl.when(s == 0)
        def _():
            relay_y().wait_recv()
            relay_x().wait_recv()
            forward(1).start()

        @pl.when(s == 1)
        def _():
            x_second().wait_recv()
            y_second().wait_recv()
            forward(2).start()

        def before(n):
            @pl.when(n >= 2)
            def _():
                lag(s, n - 2)

            @pl.when(s > 0)
            def _():
                to_core(0, n).wait_send()

        def after(n, p):
            own[lax.rem(n, 3)] = p[:ROWS]
            psend[n] = p[ROWS:].astype(BF16)
            to_core(lax.rem(s, 2), n).start()

        phase2(s + 1, 2 * ROWS, before, after)
        return 0

    lax.fori_loop(0, 3, big, 0)

    to_partner().wait_recv()

    def hook4(t):
        @pl.when(t == 1)
        def _():
            lag(2, T2 - 2)
            lag(2, T2 - 1)

    phase1(4, xp, ROWS, hook4)

    def y_copy(n):
        cols = pl.ds(pl.multiple_of(n * N2, N2), N2)
        return pltpu.make_async_copy(precv.at[1, n], y_hbm.at[:, cols], s_y.at[n])

    def final(n):
        for ss in range(3):
            for sub in range(2):
                to_owner(ss, n, sub).wait_recv()
        to_core(1, n).wait_recv()
        total = acc[n] + precv[1, n].astype(F32)
        for ss in range(3):
            total = total + rbuf[ss, n].astype(F32)
        precv[1, n] = total.astype(BF16)
        y_copy(n).start()

    def before4(n):
        @pl.when(n >= 2)
        def _():
            final(n - 2)

        to_core(1, n).wait_send()

    def after4(n, p):
        psend[n] = p.astype(BF16)
        to_core(1, n).start()

    phase2(4, ROWS, before4, after4)
    final(T2 - 2)
    final(T2 - 1)

    for c in (to_partner, x_first, y_first, relay_y, relay_x, x_second, y_second):
        c().wait_send()
    for s in range(3):
        forward(s).wait_send()

    def drain(n, _):
        to_core(1, n).wait_send()
        for s in range(3):
            for sub in range(2):
                to_owner(s, n, sub).wait_send()
        y_copy(n).wait()
        return 0

    lax.fori_loop(0, T2, drain, 0)


def solution(mesh):
    hbm = pl.BlockSpec(memory_space=pl.ANY)
    dma = pltpu.SemaphoreType.DMA

    def step(x, w_gate, w_up, w_down):
        return pl.pallas_call(
            kernel,
            out_shape=jax.ShapeDtypeStruct((ROWS, D), BF16),
            in_specs=[hbm] * 4,
            out_specs=hbm,
            scratch_shapes=[
                pltpu.VMEM((ROWS, D), BF16),
                pltpu.VMEM((ROWS, D), BF16),
                pltpu.VMEM((3, 2 * ROWS, D), BF16),
                pltpu.VMEM((2 * ROWS, FF), BF16),
                pltpu.VMEM((R1, D, N1), BF16),
                pltpu.VMEM((R1, D, N1), BF16),
                pltpu.VMEM((R2, FF, N2), BF16),
                pltpu.VMEM((T2, ROWS, N2), F32),
                pltpu.VMEM((3, ROWS, N2), F32),
                pltpu.VMEM((T2, ROWS, N2), BF16),
                pltpu.VMEM((2, T2, ROWS, N2), BF16),
                pltpu.VMEM((3, T2, ROWS, N2), BF16),
                dma, dma((R1,)), dma((R1,)), dma((R2,)), dma((T2,)),
                dma((7,)), dma((7,)), dma((3,)), dma((3,)),
                dma((T2,)), dma((2, T2)), dma((3, 2, T2)), dma((3, 2, T2)),
            ],
            compiler_params=pltpu.CompilerParams(
                collective_id=0, has_side_effects=True, vmem_limit_bytes=67043328
            ),
            cost_estimate=pl.CostEstimate(
                flops=6 * 8 * ROWS * D * FF, bytes_accessed=5 * 6 * D * FF, transcendentals=8 * ROWS * FF
            ),
            name="mlp",
        )(x, w_gate, w_up, w_down)

    return jax.shard_map(
        step,
        mesh=mesh,
        in_specs=(P(("dp", "tp"), None), P(None, "tp"), P(None, "tp"), P("tp", None)),
        out_specs=P(("dp", "tp"), None),
        check_vma=False,
    )
```

time: 414 us -> 200 us (0.48)
  waiting for transfers between devices: 201 us -> 0 us
  matrix products: 199 us -> 0 us
  Pallas kernels: 0 us -> 197 us
  between operations: 13.4 us -> 0.01 us
    dot_general x3 -> x0, matrix products: 199 us -> none  [the longest x1 74 us: step(): up = jnp.dot(rows, w_up, preferred_element_type=jnp.float32)]
    pallas_call x0 -> x1, Pallas kernels: none -> 197 us  [step(): pl.pallas_call(kernel, out_shape=jax.ShapeDtypeStruct((ROWS, D), BF16), i...]
    reduce_scatter x1 -> x0, waiting for transfers between devices: 110 us -> none  [step(): return lax.psum_scatter(term, 'tp', scatter_dimension=0, tiled=True)]
    all_gather x1 -> x0, waiting for transfers between devices: 91 us -> none  [step(): rows = lax.all_gather(x, 'tp', axis=0, tiled=True)]
  transfers between devices with their start and end apart: 2 -> 0, of which waited for: 2 -> 0; matrix products, arithmetic and copies ran while one was open for 0% -> 0% of each run, Pallas kernels for 0% -> 0%
where the time goes in v1:
time: 200 us
  Pallas kernels  197 us (98%)
  local copies, waits for them, and re-layouts  3.09 us (2%)
    pallas_call x1, Pallas kernels, step(): pl.pallas_call(kernel, out_shape=jax.ShapeDtypeStruct((ROWS, D), BF16), i...  197 us

profile of v1, /device:TPU:0, one launch (start us, length us, event | category | flops | bytes accessed | tf_op | source)
XLA Modules:
  0.0 199.9 jit_solution(8886062720763774425)
XLA Ops:
  0.0 196.8 %mlp.1 = bf16[352,3072]{1,0:T(8,128)(2,1)} custom-call(bf16[352,3072]{1,0:T(8,128)(2,1)} %x_hbm.1, bf16[3072,3072]{1,0:T(8,128)(2,1)} %wg.1, bf16[3072,3072]{1,0:T(8,128)(2,1)} %wu.1, bf16[3072,3072]{1,0:T(8,128)(2,1)} %wd.1), custom_call_target="tpu_custom_call" | custom-call | flops 159450660864 | bytes 283115520 | tf_op jit(solution)/shard_map/mlp/pallas_call | solution.py:268
  196.8 3.1 %copy.6 = bf16[352,3072]{1,0:T(8,128)(2,1)} copy(bf16[352,3072]{1,0:T(8,128)(2,1)} %mlp.1) | data formatting | bytes 4325376
